TPU v7x, 32 devices: a whole 2x2x4 slice. The times are simulated.
32 devices in a mesh: dp: 16 (over z, y, core), mp: 2 (over x).
Axes of the slice: x: 2, y: 2, z: 4, core: 2. Of those that a mesh axis runs over, the one named last changes fastest.
Arguments:
- hidden: bfloat16 [512, 7168], P('dp', 'mp'), may hold values from -12 to 12
- steering: float32 [7168], P('mp'), may hold values from -3 to 3
- norm_gain: bfloat16 [7168], P('mp'), may hold values from 0.099609375 to 1.8984375
- target: bfloat16 [512, 7168], P('dp', 'mp'), may hold values from -8 to 8
- routes: int32 [512, 8], P('dp'), may hold values from 0 to 15, all different within a row; in each aligned block of 32 rows (0 to 31, 32 to 63, ...) at most 20 rows name the same one
- gate_probs: float32 [512, 8], P('dp'), may hold values from 0.05 to 0.3
- contrast: int32 [512], P('dp'), may hold values from 0 to 1
- gate_weight: bfloat16 [16, 7168, 2048], P('dp', None, 'mp'), may hold values from -0.0625 to 0.0625
- up_weight: bfloat16 [16, 7168, 2048], P('dp', None, 'mp'), may hold values from -0.0625 to 0.0625
- down_weight: bfloat16 [16, 2048, 7168], P('dp', 'mp'), may hold values from -0.125 to 0.125
Outputs:
- mixed: bfloat16 [512, 7168], P('dp', 'mp')
- steer_grad: float32 [7168], P('mp')
Inputs may be any that keep to these rules, and one draw needn't show every extreme that they name: `routes`: each row names 8 different experts; among the 32 rows of one index of dp no expert is named by more than 20 rows.
All inputs are finite; a program needn't handle non-finite values.
Results may differ from a plain program's by a relative error of at most 0.005.
Values may be sent and summed in bfloat16 or wider, within the bound.
No kernel may reach another device: no remote copies, remote signals or barrier semaphores. Data moves between devices by JAX's collectives and lax.ppermute only.
A program may use at most 128 MiB of HBM per device.

v0:
```python
import jax
import jax.numpy as jnp
from jax import lax
from jax.sharding import PartitionSpec as P

EPSILON = 1e-06


def expert_inputs(rows_in, grad_in, gate_mat, up_mat, down_mat):
    gate_pre = jnp.einsum("secd,edf->secf", rows_in, gate_mat, preferred_element_type=jnp.float32)
    up_pre = jnp.einsum("secd,edf->secf", rows_in, up_mat, preferred_element_type=jnp.float32)
    back_hidden = jnp.einsum(
        "secd,efd->secf", grad_in, down_mat, preferred_element_type=jnp.float32
    )
    return (gate_pre, up_pre, back_hidden)


def expert_outputs(gate_pre, up_pre, back_hidden, gate_mat, up_mat, down_mat):
    sigma_gate = jax.nn.sigmoid(gate_pre)
    activated = (gate_pre * sigma_gate * up_pre).astype(jnp.bfloat16)
    grad_gate = (back_hidden * up_pre * sigma_gate * (1.0 + gate_pre * (1.0 - sigma_gate))).astype(
        jnp.bfloat16
    )
    grad_up = (back_hidden * gate_pre * sigma_gate).astype(jnp.bfloat16)
    out_part = jnp.einsum(
        "secf,efd->secd", activated, down_mat, preferred_element_type=jnp.float32
    ).astype(jnp.bfloat16)
    grad_part = (
        jnp.einsum("secf,edf->secd", grad_gate, gate_mat, preferred_element_type=jnp.float32)
        + jnp.einsum("secf,edf->secd", grad_up, up_mat, preferred_element_type=jnp.float32)
    ).astype(jnp.bfloat16)
    return (out_part, grad_part)


def body(
    hidden,
    steering,
    norm_gain,
    target,
    routes,
    gate_probs,
    contrast,
    gate_weight,
    up_weight,
    down_weight,
):
    tokens_here, width_here = hidden.shape
    groups = lax.axis_size("dp")
    quarters = lax.axis_size("mp")
    local_experts = gate_weight.shape[0]
    experts_all = local_experts * groups
    top_count = routes.shape[1]
    capacity = min(
        tokens_here, (5 * tokens_here * top_count + 4 * experts_all - 1) // (4 * experts_all)
    )
    pair_count = tokens_here * top_count
    slot_count = experts_all * capacity
    width_full = width_here * quarters
    stream = hidden.astype(jnp.float32) + steering[None, :]
    square_sum = lax.psum(jnp.sum(stream * stream, axis=1), "mp")
    inverse = lax.rsqrt(square_sum / width_full + EPSILON)[:, None]
    gain_row = norm_gain.astype(jnp.float32)[None, :]
    normed = (stream * inverse * gain_row).astype(jnp.bfloat16)
    sign_col = (2 * contrast - 1).astype(jnp.float32)[:, None]
    flat_routes = routes.reshape(-1)
    one_hot = (flat_routes[:, None] == jnp.arange(experts_all, dtype=jnp.int32)[None, :]).astype(
        jnp.int32
    )
    earlier = jnp.cumsum(one_hot, axis=0) - one_hot
    rank_in = jnp.sum(earlier * one_hot, axis=1)
    slot_of = flat_routes * capacity + rank_in
    source = (
        jnp.full((slot_count,), pair_count, jnp.int32)
        .at[slot_of]
        .set(jnp.arange(pair_count, dtype=jnp.int32))
    )
    source_tok = source // top_count
    probs_pad = jnp.concatenate([gate_probs.reshape(-1), jnp.zeros((1,), jnp.float32)])
    slot_probs = probs_pad[source][:, None]
    col_count = normed.shape[1]
    rows_pad = jnp.concatenate([normed, jnp.zeros((1, col_count), jnp.bfloat16)], axis=0)
    cot_pad = jnp.concatenate(
        [target.astype(jnp.float32) * sign_col, jnp.zeros((1, col_count), jnp.float32)], axis=0
    )
    send_rows = rows_pad[source_tok].reshape(groups, local_experts, capacity, col_count)
    send_grad = (
        (cot_pad[source_tok] * slot_probs)
        .astype(jnp.bfloat16)
        .reshape(groups, local_experts, capacity, col_count)
    )
    send_rows, send_grad = (send_rows, send_grad)
    rows_in = lax.all_to_all(send_rows, "dp", split_axis=0, concat_axis=0, tiled=True)
    grad_in = lax.all_to_all(send_grad, "dp", split_axis=0, concat_axis=0, tiled=True)
    zeros_init = jnp.zeros(rows_in.shape[:3] + (gate_weight.shape[2],), jnp.float32)
    rows_piece = lax.all_gather(rows_in, "mp", axis=3, tiled=True)
    grad_piece = lax.all_gather(grad_in, "mp", axis=3, tiled=True)
    partial_terms = expert_inputs(rows_piece, grad_piece, gate_weight, up_weight, down_weight)
    gate_pre, up_pre, back_hidden = jax.tree.map(
        jnp.add, (zeros_init, zeros_init, zeros_init), partial_terms
    )
    out_part, grad_part = expert_outputs(
        gate_pre, up_pre, back_hidden, gate_weight, up_weight, down_weight
    )
    out_share = lax.psum_scatter(
        out_part.astype(jnp.float32).astype(jnp.bfloat16), "mp", scatter_dimension=3, tiled=True
    ).astype(jnp.float32)
    grad_share = lax.psum_scatter(
        grad_part.astype(jnp.float32).astype(jnp.bfloat16), "mp", scatter_dimension=3, tiled=True
    ).astype(jnp.float32)
    back_out = lax.all_to_all(
        out_share.astype(jnp.bfloat16), "dp", split_axis=0, concat_axis=0, tiled=True
    ).astype(out_share.dtype)
    back_grad = lax.all_to_all(
        grad_share.astype(jnp.bfloat16), "dp", split_axis=0, concat_axis=0, tiled=True
    ).astype(grad_share.dtype)
    col_count = back_out.shape[3]
    out_slots = back_out.reshape(slot_count, col_count)[slot_of].reshape(
        tokens_here, top_count, col_count
    )
    grad_slots = back_grad.reshape(slot_count, col_count)[slot_of].reshape(
        tokens_here, top_count, col_count
    )
    out_tok = jnp.sum(out_slots * gate_probs[:, :, None], axis=1)
    grad_tok = jnp.sum(grad_slots, axis=1)
    mixed = (stream + out_tok).astype(jnp.bfloat16)
    project = lax.psum(jnp.sum(stream * gain_row * grad_tok, axis=1), "mp")[:, None]
    cotangent = target.astype(jnp.float32) * sign_col
    grad_stream = (
        cotangent
        + inverse * gain_row * grad_tok
        - stream * inverse * inverse * inverse * project / width_full
    )
    steer_grad = lax.psum(jnp.sum(grad_stream, axis=0), "dp")
    return (mixed, steer_grad)


def solution(mesh):
    placed = (
        P("dp", "mp"),
        P("mp"),
        P("mp"),
        P("dp", "mp"),
        P("dp", None),
        P("dp", None),
        P("dp"),
        P("dp", None, "mp"),
        P("dp", None, "mp"),
        P("dp", "mp", None),
    )
    return jax.shard_map(
        body, mesh=mesh, in_specs=placed, out_specs=(P("dp", "mp"), P("mp")), check_vma=False
    )
```

profile of v0, /device:TPU:0, one launch (start us, length us, event | category | flops | bytes accessed | tf_op | source)
XLA Modules:
  0.0 593.2 jit_solution(3055648589652543636)
XLA Ops:
  9.9 1.4 scatter_custom_fusion
  13.1 4.1 gather_fusion.2
  17.1 5.2 gather.20
  22.5 2.4 gather_fusion.3
  25.1 4.7 fusion.27
  29.8 7.5 %all-to-all-start.2 = ((bf16[16,1,20,3584]{3,2,1,0:T(8,128)(2,1)}), bf16[16,1,20,3584]{3,2,1,0:T(8,128)(2,1)S(1)}, u32[]{:S(2)}, u32[]{:S(2)}) async-start(bf16[16,1,20,3584]{3,2,1,0:T(8,128)(2,1)} %fusion.27), calls=%async_computation.3 | async-start | bytes 5505024 | tf_op jit(solution)/shard_map/all_to_all | solution.py:93
  37.7 4.9 psum.21
  42.6 47.2 %all-to-all-done.2 = bf16[16,1,20,3584]{3,2,1,0:T(8,128)(2,1)S(1)} async-done(((bf16[16,1,20,3584]{3,2,1,0:T(8,128)(2,1)}), bf16[16,1,20,3584]{3,2,1,0:T(8,128)(2,1)S(1)}, u32[]{:S(2)}, u32[]{:S(2)}) %all-to-all-start.2) | async-done | bytes 2293792 | tf_op jit(solution)/shard_map/all_to_all | solution.py:93
  89.8 1.5 copy-done
  91.5 3.7 gather_fusion
  95.2 2.6 reshape.140
  97.8 77.0 %all_to_all.20 = bf16[16,1,20,3584]{3,2,1,0:T(8,128)(2,1)} all-to-all(bf16[16,1,20,3584]{3,2,1,0:T(8,128)(2,1)S(1)} %bitcast.165), channel_id=1, replica_groups=mesh['dp'=16,'mp'=2] {'dp'}, dimensions={0} | all-to-all | bytes 4587520 | tf_op jit(solution)/shard_map/all_to_all | solution.py:92
  175.1 11.8 %fusion = f32[16,20,1024]{2,1,0:T(8,128)} fusion(bf16[1,1024,7168]{2,1,0:T(8,128)(2,1)} %param.19, bf16[16,1,20,7168]{3,2,0,1:T(8,128)(2,1)} %all-gather.5.cloned.1.call-done), kind=kOutput, calls=%fused_computation.6 | convolution fusion | flops 4697620480 | bytes 20578304 | tf_op jit(solution)/shard_map/secd,efd->secf/dot_general | solution.py:12
  186.9 58.3 %all-gather.3.cloned.1.call-done = bf16[16,1,20,7168]{3,2,0,1:T(8,128)(2,1)} async-done(((bf16[16,1,20,3584]{3,2,0,1:T(8,128)(2,1)}), bf16[16,1,20,7168]{3,2,0,1:T(8,128)(2,1)}) %all-gather.3.cloned.1.call-update) | async-done | bytes 4587536 | tf_op jit(solution)/shard_map/all_gather | solution.py:95
  245.2 10.9 %fusion.10 = f32[16,20,1024]{2,1,0:T(8,128)S(1)} fusion(bf16[1,7168,1024]{2,1,0:T(8,128)(2,1)} %param.17, bf16[16,1,20,7168]{3,2,0,1:T(8,128)(2,1)} %all-gather.3.cloned.1.call-done), kind=kOutput, calls=%fused_computation.16 | convolution fusion | flops 4697620480 | bytes 20578304 | tf_op jit(solution)/shard_map/secd,edf->secf/dot_general | solution.py:10
  256.2 22.0 %fusion.4 = f32[16,20,7168]{2,1,0:T(8,128)} fusion(bf16[1,7168,1024]{2,1,0:T(8,128)(2,1)} %param.18, f32[16,20,1024]{2,1,0:T(8,128)S(1)} %copy-done.7, f32[16,20,1024]{2,1,0:T(8,128)S(1)} %fusion.10), kind=kOutput, calls=%fused_computation.10 | convolution fusion | flops 4699586560 | bytes 26476544 | tf_op jit(solution)/shard_map/secf,edf->secd/dot_general | solution.py:30
  278.2 10.4 %fusion.6 = f32[16,20,1024]{2,1,0:T(8,128)} fusion(bf16[1,7168,1024]{2,1,0:T(8,128)(2,1)} %param.18, bf16[16,1,20,7168]{3,2,0,1:T(8,128)(2,1)S(1)} %copy-done.6), kind=kOutput, calls=%fused_computation.12 | convolution fusion | flops 4697620480 | bytes 20578304 | tf_op jit(solution)/shard_map/secd,edf->secf/dot_general | solution.py:11
  288.6 14.2 %fusion.20 = bf16[16,1,20,7168]{3,2,0,1:T(8,128)(2,1)} fusion(f32[16,20,7168]{2,1,0:T(8,128)} %fusion.4, bf16[1,7168,1024]{2,1,0:T(8,128)(2,1)} %param.17, f32[16,20,1024]{2,1,0:T(8,128)} %fusion, f32[16,20,1024]{2,1,0:T(8,128)} %fusion.6, f32[16,20,1024]{2,1,0:T(8,128)S(1)} %fusion.10), kind=kOutput, calls=%fused_computation.21 | convolution fusion | flops 4705484800 | bytes 32374784 | tf_op jit(solution)/shard_map/secf,edf->secd/dot_general | solution.py:29
  302.8 11.4 %fusion.17 = bf16[16,1,20,7168]{3,2,0,1:T(8,128)(2,1)} fusion(bf16[1,1024,7168]{2,1,0:T(8,128)(2,1)} %param.19, f32[16,20,1024]{2,1,0:T(8,128)} %fusion.6, f32[16,20,1024]{2,1,0:T(8,128)S(1)} %fusion.10), kind=kOutput, calls=%fused_computation.20 | convolution fusion | flops 4701880320 | bytes 21889024 | tf_op jit(solution)/shard_map/secf,efd->secd/dot_general | solution.py:25
  314.3 57.3 %reduce-scatter.5.cloned.1.call-done = bf16[16,1,20,3584]{3,2,0,1:T(8,128)(2,1)} async-done(((bf16[16,1,20,7168]{3,2,0,1:T(8,128)(2,1)}), bf16[16,1,20,3584]{3,2,0,1:T(8,128)(2,1)}) %reduce-scatter.5.cloned.1.call-update) | async-done | bytes 2293776 | tf_op jit(solution)/shard_map/reduce_scatter | solution.py:107
  371.6 5.6 all-to-all-start.3
  377.2 65.2 %reduce-scatter.3.cloned.1.call-done = bf16[16,1,20,3584]{3,2,0,1:T(8,128)(2,1)} async-done(((bf16[16,1,20,7168]{3,2,0,1:T(8,128)(2,1)}), bf16[16,1,20,3584]{3,2,0,1:T(8,128)(2,1)}) %reduce-scatter.3.cloned.1.call-update) | async-done | bytes 2293776 | tf_op jit(solution)/shard_map/reduce_scatter | solution.py:104
  442.3 5.7 all-to-all-start.1
  448.1 2.6 reshape.159
  450.7 7.5 %gather_fusion.4 = f32[256,3584]{1,0:T(8,128)} fusion(f32[320,3584]{1,0:T(8,128)} %reshape.159, s32[1024]{0:T(1024)S(1)} %pad_clamp_fusion.1), kind=kCustom, calls=%fused_computation.4 | custom fusion | bytes 7341056 | tf_op jit(solution)/shard_map/gather | solution.py:120
  458.2 3.0 bitcast_reduce_fusion
  461.3 4.9 psum.22
  466.3 34.2 %all-to-all-done.1 = bf16[16,1,20,3584]{3,2,1,0:T(8,128)(2,1)} async-done(((bf16[16,1,20,3584]{3,2,1,0:T(8,128)(2,1)}), bf16[16,1,20,3584]{3,2,1,0:T(8,128)(2,1)}, u32[]{:S(2)}, u32[]{:S(2)}) %all-to-all-start.1) | async-done | bytes 2293792 | tf_op jit(solution)/shard_map/all_to_all | solution.py:110
  500.5 4.5 reshape.157
  505.0 7.5 %gather_fusion.1 = f32[256,3584]{1,0:T(8,128)} fusion(f32[320,3584]{1,0:T(8,128)} %reshape.157, s32[1024]{0:T(1024)S(1)} %pad_clamp_fusion.1), kind=kCustom, calls=%fused_computation.1 | custom fusion | bytes 7341056 | tf_op jit(solution)/shard_map/gather | solution.py:117
  512.4 3.3 fusion.26
  516.7 70.0 %psum.23 = f32[3584]{0:T(1024)} all-reduce(f32[3584]{0:T(1024)S(1)} %get-tuple-element.2), channel_id=1, replica_groups=mesh['dp'=16,'mp'=2] {'dp'}, use_global_device_ids=true, to_apply=%region_13.14 | all-reduce | flops 3584 | bytes 28672 | tf_op jit(solution)/shard_map/psum | solution.py:133
  (56 shorter events, 6.7 us)
Async XLA Ops:
  17.1 5.2 copy-start.5
  29.8 7.6 %copy-start.4 = (bf16[3584]{0:T(1024)(128)(2,1)S(1)}, bf16[3584]{0:T(1024)(128)(2,1)}, u32[]{:S(2)}) copy-start(bf16[3584]{0:T(1024)(128)(2,1)} %param.12) | copy-start | bytes 21508
  29.8 7.6 %copy-start.1 = (bf16[32,3584]{1,0:T(8,128)(2,1)S(1)}, bf16[32,3584]{1,0:T(8,128)(2,1)}, u32[]{:S(2)}) copy-start(bf16[32,3584]{1,0:T(8,128)(2,1)} %param.10) | copy-start | bytes 688132
  29.8 7.6 %copy-start.3 = (f32[3584]{0:T(1024)S(1)}, f32[3584]{0:T(1024)}, u32[]{:S(2)}) copy-start(f32[3584]{0:T(1024)} %param.11) | copy-start | bytes 43012
  29.8 59.9 %all-to-all-start.2 = ((bf16[16,1,20,3584]{3,2,1,0:T(8,128)(2,1)}), bf16[16,1,20,3584]{3,2,1,0:T(8,128)(2,1)S(1)}, u32[]{:S(2)}, u32[]{:S(2)}) async-start(bf16[16,1,20,3584]{3,2,1,0:T(8,128)(2,1)} %fusion.27), calls=%async_computation.3 | async-start | bytes 5505024 | tf_op jit(solution)/shard_map/all_to_all | solution.py:93
  37.4 137.7 %all-gather.5.cloned.1.call-start = ((), (), s32[]{:S(2)}) async-start(), calls=%async_computation.8 | async-start | bytes 8257536 | tf_op jit(solution)/shard_map/all_gather | solution.py:96
  89.8 1.5 copy-start
  91.3 153.9 %all-gather.3.cloned.1.call-start = ((), (), s32[]{:S(2)}) async-start(), calls=%async_computation.6 | async-start | bytes 8257536 | tf_op jit(solution)/shard_map/all_gather | solution.py:95
  174.8 196.8 %reduce-scatter.5.cloned.1.call-start = ((), (), s32[]{:S(2)}) async-start(), calls=%async_computation.9 | async-start | bytes 8257536 | tf_op jit(solution)/shard_map/reduce_scatter | solution.py:107
  245.2 10.9 %copy-start.7 = (f32[16,20,1024]{2,1,0:T(8,128)S(1)}, f32[16,20,1024]{2,1,0:T(8,128)}, u32[]{:S(2)}) copy-start(f32[16,20,1024]{2,1,0:T(8,128)} %fusion) | copy-start | bytes 3932164
  256.2 22.0 %copy-start.6 = (bf16[16,1,20,7168]{3,2,0,1:T(8,128)(2,1)S(1)}, bf16[16,1,20,7168]{3,2,0,1:T(8,128)(2,1)}, u32[]{:S(2)}) copy-start(bf16[16,1,20,7168]{3,2,0,1:T(8,128)(2,1)} %all-gather.3.cloned.1.call-done) | copy-start | bytes 13762564
  302.8 139.6 %reduce-scatter.3.cloned.1.call-start = ((), (), s32[]{:S(2)}) async-start(), calls=%async_computation.7 | async-start | bytes 8257536 | tf_op jit(solution)/shard_map/reduce_scatter | solution.py:104
  371.6 70.8 %all-to-all-start.3 = ((bf16[16,1,20,3584]{3,2,1,0:T(8,128)(2,1)}), bf16[16,1,20,3584]{3,2,1,0:T(8,128)(2,1)S(1)}, u32[]{:S(2)}, u32[]{:S(2)}) async-start(bf16[16,1,20,3584]{3,2,1,0:T(8,128)(2,1)} %bitcast.167), calls=%async_computation.5 | async-start | bytes 5505024 | tf_op jit(solution)/shard_map/all_to_all | solution.py:113
  442.3 58.1 %all-to-all-start.1 = ((bf16[16,1,20,3584]{3,2,1,0:T(8,128)(2,1)}), bf16[16,1,20,3584]{3,2,1,0:T(8,128)(2,1)}, u32[]{:S(2)}, u32[]{:S(2)}) async-start(bf16[16,1,20,3584]{3,2,1,0:T(8,128)(2,1)} %bitcast.166), calls=%async_computation.2 | async-start | bytes 5505024 | tf_op jit(solution)/shard_map/all_to_all | solution.py:110
  512.4 3.3 copy-start.2
Sparse Core Ops, SparseCore 0:
  91.4 80.6 all-gather.4
  174.9 70.2 all-gather.2
  302.9 68.6 reduce-scatter.4
  373.7 68.5 reduce-scatter.2
where the time goes:
time: 594 us; the launch traced here: 593 us
  waiting for transfers between devices  262 us (44%)
  blocking collectives  157 us (26%)
  matrix products  80.7 us (14%)
  local copies, waits for them, and re-layouts  44.6 us (8%)
  starting transfers between devices  19.2 us (3%)
  other arithmetic  15.6 us (3%)
  between operations  14 us (2%)
    all_to_all x1, blocking collectives, body(): lax.all_to_all(send_rows, 'dp', split_axis=0, concat_axis=0, tiled=True)  77 us
    psum x1, blocking collectives, body(): steer_grad = lax.psum(jnp.sum(grad_stream, axis=0), 'dp')  70 us
    reduce_scatter x1, waiting for transfers between devices, body(): lax.psum_scatter(out_part.astype(jnp.float32).astype(jnp.bfloat16), 'mp',...  65.2 us
    all_gather x1, waiting for transfers between devices, body(): rows_piece = lax.all_gather(rows_in, 'mp', axis=3, tiled=True)  58.3 us
    reduce_scatter x1, waiting for transfers between devices, body(): lax.psum_scatter(grad_part.astype(jnp.float32).astype(jnp.bfloat16), 'mp'...  57.3 us
    all_to_all x1, waiting for transfers between devices, body(): lax.all_to_all(send_grad, 'dp', split_axis=0, concat_axis=0, tiled=True)  47.2 us
    all_to_all x1, waiting for transfers between devices, body(): lax.all_to_all(out_share.astype(jnp.bfloat16), 'dp', split_axis=0, concat...  34.2 us
    dot_general x1, matrix products, expert_outputs(): jnp.einsum('secf,edf->secd', grad_up, up_mat, preferred_element_type=jnp....  22 us
  transfers between devices with their start and end apart: 7, of which 5 were waited for; matrix products, arithmetic and copies ran while one was open for 7% of the time, Pallas kernels for 0%

commit v1 on v0

--- a/solution.py
+++ b/solution.py
@@ -130,7 +130,7 @@
         + inverse * gain_row * grad_tok
         - stream * inverse * inverse * inverse * project / width_full
     )
-    steer_grad = lax.psum(jnp.sum(grad_stream, axis=0), "dp")
+    steer_grad = jnp.sum(lax.all_gather(jnp.sum(grad_stream, axis=0), "dp"), axis=0)
     return (mixed, steer_grad)
 
 

time: 594 us -> 555 us (0.934)
  blocking collectives: 157 us -> 117 us
    psum x1 -> x0, blocking collectives: 70 us -> none  [body(): steer_grad = lax.psum(jnp.sum(grad_stream, axis=0), 'dp')]
    all_gather x0 -> x1, blocking collectives: none -> 30.2 us  [body(): lax.all_gather(jnp.sum(grad_stream, axis=0), 'dp')]
  transfers between devices with their start and end apart: 7 -> 7, of which waited for: 5 -> 5; matrix products, arithmetic and copies ran while one was open for 7% -> 8% of each run, Pallas kernels for 0% -> 0%
where the time goes in v1:
time: 555 us; the launch traced here: 554 us
  waiting for transfers between devices  262 us (47%)
  blocking collectives  117 us (21%)
  matrix products  80.7 us (15%)
  local copies, waits for them, and re-layouts  44.6 us (8%)
  starting transfers between devices  19.2 us (3%)
  other arithmetic  16.3 us (3%)
  between operations  14 us (3%)
    all_to_all x1, blocking collectives, body(): lax.all_to_all(send_rows, 'dp', split_axis=0, concat_axis=0, tiled=True)  77 us
    reduce_scatter x1, waiting for transfers between devices, body(): lax.psum_scatter(out_part.astype(jnp.float32).astype(jnp.bfloat16), 'mp',...  65.2 us
    all_gather x1, waiting for transfers between devices, body(): rows_piece = lax.all_gather(rows_in, 'mp', axis=3, tiled=True)  58.3 us
    reduce_scatter x1, waiting for transfers between devices, body(): lax.psum_scatter(grad_part.astype(jnp.float32).astype(jnp.bfloat16), 'mp'...  57.3 us
    all_to_all x1, waiting for transfers between devices, body(): lax.all_to_all(send_grad, 'dp', split_axis=0, concat_axis=0, tiled=True)  47.2 us
    all_to_all x1, waiting for transfers between devices, body(): lax.all_to_all(out_share.astype(jnp.bfloat16), 'dp', split_axis=0, concat...  34.2 us
    all_gather x1, blocking collectives, body(): lax.all_gather(jnp.sum(grad_stream, axis=0), 'dp')  30.2 us
    dot_general x1, matrix products, expert_outputs(): jnp.einsum('secf,edf->secd', grad_up, up_mat, preferred_element_type=jnp....  22 us
  transfers between devices with their start and end apart: 7, of which 5 were waited for; matrix products, arithmetic and copies ran while one was open for 8% of the time, Pallas kernels for 0%

profile of v1, /device:TPU:0, one launch (start us, length us, event | category | flops | bytes accessed | tf_op | source)
XLA Modules:
  0.0 554.2 jit_solution(13382897888338173206)
XLA Ops:
  9.9 1.4 scatter_custom_fusion
  13.1 4.1 gather_fusion.2
  17.1 5.2 gather.20
  22.5 2.4 gather_fusion.3
  25.1 4.7 fusion.27
  29.8 7.5 %all-to-all-start.2 = ((bf16[16,1,20,3584]{3,2,1,0:T(8,128)(2,1)}), bf16[16,1,20,3584]{3,2,1,0:T(8,128)(2,1)S(1)}, u32[]{:S(2)}, u32[]{:S(2)}) async-start(bf16[16,1,20,3584]{3,2,1,0:T(8,128)(2,1)} %fusion.27), calls=%async_computation.3 | async-start | bytes 5505024 | tf_op jit(solution)/shard_map/all_to_all | solution.py:93
  37.7 4.9 psum.14
  42.6 47.2 %all-to-all-done.2 = bf16[16,1,20,3584]{3,2,1,0:T(8,128)(2,1)S(1)} async-done(((bf16[16,1,20,3584]{3,2,1,0:T(8,128)(2,1)}), bf16[16,1,20,3584]{3,2,1,0:T(8,128)(2,1)S(1)}, u32[]{:S(2)}, u32[]{:S(2)}) %all-to-all-start.2) | async-done | bytes 2293792 | tf_op jit(solution)/shard_map/all_to_all | solution.py:93
  89.8 1.5 copy-done
  91.5 3.7 gather_fusion
  95.2 2.6 reshape.140
  97.8 77.0 %all_to_all.20 = bf16[16,1,20,3584]{3,2,1,0:T(8,128)(2,1)} all-to-all(bf16[16,1,20,3584]{3,2,1,0:T(8,128)(2,1)S(1)} %bitcast.165), channel_id=1, replica_groups=mesh['dp'=16,'mp'=2] {'dp'}, dimensions={0} | all-to-all | bytes 4587520 | tf_op jit(solution)/shard_map/all_to_all | solution.py:92
  175.1 11.8 %fusion = f32[16,20,1024]{2,1,0:T(8,128)} fusion(bf16[1,1024,7168]{2,1,0:T(8,128)(2,1)} %param.19, bf16[16,1,20,7168]{3,2,0,1:T(8,128)(2,1)} %all-gather.7.cloned.1.call-done), kind=kOutput, calls=%fused_computation.6 | convolution fusion | flops 4697620480 | bytes 20578304 | tf_op jit(solution)/shard_map/secd,efd->secf/dot_general | solution.py:12
  186.9 58.3 %all-gather.5.cloned.1.call-done = bf16[16,1,20,7168]{3,2,0,1:T(8,128)(2,1)} async-done(((bf16[16,1,20,3584]{3,2,0,1:T(8,128)(2,1)}), bf16[16,1,20,7168]{3,2,0,1:T(8,128)(2,1)}) %all-gather.5.cloned.1.call-update) | async-done | bytes 4587536 | tf_op jit(solution)/shard_map/all_gather | solution.py:95
  245.2 10.9 %fusion.10 = f32[16,20,1024]{2,1,0:T(8,128)S(1)} fusion(bf16[1,7168,1024]{2,1,0:T(8,128)(2,1)} %param.17, bf16[16,1,20,7168]{3,2,0,1:T(8,128)(2,1)} %all-gather.5.cloned.1.call-done), kind=kOutput, calls=%fused_computation.16 | convolution fusion | flops 4697620480 | bytes 20578304 | tf_op jit(solution)/shard_map/secd,edf->secf/dot_general | solution.py:10
  256.2 22.0 %fusion.4 = f32[16,20,7168]{2,1,0:T(8,128)} fusion(bf16[1,7168,1024]{2,1,0:T(8,128)(2,1)} %param.18, f32[16,20,1024]{2,1,0:T(8,128)S(1)} %copy-done.7, f32[16,20,1024]{2,1,0:T(8,128)S(1)} %fusion.10), kind=kOutput, calls=%fused_computation.10 | convolution fusion | flops 4699586560 | bytes 26476544 | tf_op jit(solution)/shard_map/secf,edf->secd/dot_general | solution.py:30
  278.2 10.4 %fusion.6 = f32[16,20,1024]{2,1,0:T(8,128)} fusion(bf16[1,7168,1024]{2,1,0:T(8,128)(2,1)} %param.18, bf16[16,1,20,7168]{3,2,0,1:T(8,128)(2,1)S(1)} %copy-done.6), kind=kOutput, calls=%fused_computation.12 | convolution fusion | flops 4697620480 | bytes 20578304 | tf_op jit(solution)/shard_map/secd,edf->secf/dot_general | solution.py:11
  288.6 14.2 %fusion.20 = bf16[16,1,20,7168]{3,2,0,1:T(8,128)(2,1)} fusion(f32[16,20,7168]{2,1,0:T(8,128)} %fusion.4, bf16[1,7168,1024]{2,1,0:T(8,128)(2,1)} %param.17, f32[16,20,1024]{2,1,0:T(8,128)} %fusion, f32[16,20,1024]{2,1,0:T(8,128)} %fusion.6, f32[16,20,1024]{2,1,0:T(8,128)S(1)} %fusion.10), kind=kOutput, calls=%fused_computation.21 | convolution fusion | flops 4705484800 | bytes 32374784 | tf_op jit(solution)/shard_map/secf,edf->secd/dot_general | solution.py:29
  302.8 11.4 %fusion.17 = bf16[16,1,20,7168]{3,2,0,1:T(8,128)(2,1)} fusion(bf16[1,1024,7168]{2,1,0:T(8,128)(2,1)} %param.19, f32[16,20,1024]{2,1,0:T(8,128)} %fusion.6, f32[16,20,1024]{2,1,0:T(8,128)S(1)} %fusion.10), kind=kOutput, calls=%fused_computation.20 | convolution fusion | flops 4701880320 | bytes 21889024 | tf_op jit(solution)/shard_map/secf,efd->secd/dot_general | solution.py:25
  314.3 57.3 %reduce-scatter.5.cloned.1.call-done = bf16[16,1,20,3584]{3,2,0,1:T(8,128)(2,1)} async-done(((bf16[16,1,20,7168]{3,2,0,1:T(8,128)(2,1)}), bf16[16,1,20,3584]{3,2,0,1:T(8,128)(2,1)}) %reduce-scatter.5.cloned.1.call-update) | async-done | bytes 2293776 | tf_op jit(solution)/shard_map/reduce_scatter | solution.py:107
  371.6 5.6 %all-to-all-start.3 = ((bf16[16,1,20,3584]{3,2,1,0:T(8,128)(2,1)}), bf16[16,1,20,3584]{3,2,1,0:T(8,128)(2,1)S(1)}, u32[]{:S(2)}, u32[]{:S(2)}) async-start(bf16[16,1,20,3584]{3,2,1,0:T(8,128)(2,1)} %bitcast.167), calls=%async_computation.5 | async-start | bytes 5505024 | tf_op jit(solution)/shard_map/all_to_all | solution.py:113
  377.2 65.2 %reduce-scatter.3.cloned.1.call-done = bf16[16,1,20,3584]{3,2,0,1:T(8,128)(2,1)} async-done(((bf16[16,1,20,7168]{3,2,0,1:T(8,128)(2,1)}), bf16[16,1,20,3584]{3,2,0,1:T(8,128)(2,1)}) %reduce-scatter.3.cloned.1.call-update) | async-done | bytes 2293776 | tf_op jit(solution)/shard_map/reduce_scatter | solution.py:104
  442.3 5.7 %all-to-all-start.1 = ((bf16[16,1,20,3584]{3,2,1,0:T(8,128)(2,1)}), bf16[16,1,20,3584]{3,2,1,0:T(8,128)(2,1)}, u32[]{:S(2)}, u32[]{:S(2)}) async-start(bf16[16,1,20,3584]{3,2,1,0:T(8,128)(2,1)} %bitcast.166), calls=%async_computation.2 | async-start | bytes 5505024 | tf_op jit(solution)/shard_map/all_to_all | solution.py:110
  448.1 2.6 reshape.159
  450.7 7.5 %gather_fusion.4 = f32[256,3584]{1,0:T(8,128)} fusion(f32[320,3584]{1,0:T(8,128)} %reshape.159, s32[1024]{0:T(1024)S(1)} %pad_clamp_fusion.1), kind=kCustom, calls=%fused_computation.4 | custom fusion | bytes 7341056 | tf_op jit(solution)/shard_map/gather | solution.py:120
  458.2 3.0 bitcast_reduce_fusion
  461.3 4.9 psum.15
  466.3 34.2 %all-to-all-done.1 = bf16[16,1,20,3584]{3,2,1,0:T(8,128)(2,1)} async-done(((bf16[16,1,20,3584]{3,2,1,0:T(8,128)(2,1)}), bf16[16,1,20,3584]{3,2,1,0:T(8,128)(2,1)}, u32[]{:S(2)}, u32[]{:S(2)}) %all-to-all-start.1) | async-done | bytes 2293792 | tf_op jit(solution)/shard_map/all_to_all | solution.py:110
  500.5 4.5 reshape.157
  505.0 7.5 %gather_fusion.1 = f32[256,3584]{1,0:T(8,128)} fusion(f32[320,3584]{1,0:T(8,128)} %reshape.157, s32[1024]{0:T(1024)S(1)} %pad_clamp_fusion.1), kind=kCustom, calls=%fused_computation.1 | custom fusion | bytes 7341056 | tf_op jit(solution)/shard_map/gather | solution.py:117
  512.4 3.3 fusion.26
  516.7 30.2 %all-gather.1 = f32[16,1,3584]{2,1,0:T(1,128)S(1)} all-gather(f32[1,1,3584]{2,1,0:T(1,128)S(1)} %reshape.212), channel_id=2, replica_groups=mesh['dp'=16,'mp'=2] {'dp'}, dimensions={0}, use_global_device_ids=true | all-gather | bytes 243712 | tf_op jit(solution)/shard_map/all_gather | solution.py:133
  (58 shorter events, 7.5 us)
Async XLA Ops:
  17.1 5.2 copy-start.5
  29.8 7.6 %copy-start.4 = (bf16[3584]{0:T(1024)(128)(2,1)S(1)}, bf16[3584]{0:T(1024)(128)(2,1)}, u32[]{:S(2)}) copy-start(bf16[3584]{0:T(1024)(128)(2,1)} %param.12) | copy-start | bytes 21508
  29.8 7.6 %copy-start.1 = (bf16[32,3584]{1,0:T(8,128)(2,1)S(1)}, bf16[32,3584]{1,0:T(8,128)(2,1)}, u32[]{:S(2)}) copy-start(bf16[32,3584]{1,0:T(8,128)(2,1)} %param.10) | copy-start | bytes 688132
  29.8 7.6 %copy-start.3 = (f32[3584]{0:T(1024)S(1)}, f32[3584]{0:T(1024)}, u32[]{:S(2)}) copy-start(f32[3584]{0:T(1024)} %param.11) | copy-start | bytes 43012
  29.8 59.9 %all-to-all-start.2 = ((bf16[16,1,20,3584]{3,2,1,0:T(8,128)(2,1)}), bf16[16,1,20,3584]{3,2,1,0:T(8,128)(2,1)S(1)}, u32[]{:S(2)}, u32[]{:S(2)}) async-start(bf16[16,1,20,3584]{3,2,1,0:T(8,128)(2,1)} %fusion.27), calls=%async_computation.3 | async-start | bytes 5505024 | tf_op jit(solution)/shard_map/all_to_all | solution.py:93
  37.4 137.7 %all-gather.7.cloned.1.call-start = ((), (), s32[]{:S(2)}) async-start(), calls=%async_computation.8 | async-start | bytes 8257536 | tf_op jit(solution)/shard_map/all_gather | solution.py:96
  89.8 1.5 copy-start
  91.3 153.9 %all-gather.5.cloned.1.call-start = ((), (), s32[]{:S(2)}) async-start(), calls=%async_computation.6 | async-start | bytes 8257536 | tf_op jit(solution)/shard_map/all_gather | solution.py:95
  174.8 196.8 %reduce-scatter.5.cloned.1.call-start = ((), (), s32[]{:S(2)}) async-start(), calls=%async_computation.9 | async-start | bytes 8257536 | tf_op jit(solution)/shard_map/reduce_scatter | solution.py:107
  245.2 10.9 %copy-start.7 = (f32[16,20,1024]{2,1,0:T(8,128)S(1)}, f32[16,20,1024]{2,1,0:T(8,128)}, u32[]{:S(2)}) copy-start(f32[16,20,1024]{2,1,0:T(8,128)} %fusion) | copy-start | bytes 3932164
  256.2 22.0 %copy-start.6 = (bf16[16,1,20,7168]{3,2,0,1:T(8,128)(2,1)S(1)}, bf16[16,1,20,7168]{3,2,0,1:T(8,128)(2,1)}, u32[]{:S(2)}) copy-start(bf16[16,1,20,7168]{3,2,0,1:T(8,128)(2,1)} %all-gather.5.cloned.1.call-done) | copy-start | bytes 13762564
  302.8 139.6 %reduce-scatter.3.cloned.1.call-start = ((), (), s32[]{:S(2)}) async-start(), calls=%async_computation.7 | async-start | bytes 8257536 | tf_op jit(solution)/shard_map/reduce_scatter | solution.py:104
  371.6 70.8 %all-to-all-start.3 = ((bf16[16,1,20,3584]{3,2,1,0:T(8,128)(2,1)}), bf16[16,1,20,3584]{3,2,1,0:T(8,128)(2,1)S(1)}, u32[]{:S(2)}, u32[]{:S(2)}) async-start(bf16[16,1,20,3584]{3,2,1,0:T(8,128)(2,1)} %bitcast.167), calls=%async_computation.5 | async-start | bytes 5505024 | tf_op jit(solution)/shard_map/all_to_all | solution.py:113
  442.3 58.1 %all-to-all-start.1 = ((bf16[16,1,20,3584]{3,2,1,0:T(8,128)(2,1)}), bf16[16,1,20,3584]{3,2,1,0:T(8,128)(2,1)}, u32[]{:S(2)}, u32[]{:S(2)}) async-start(bf16[16,1,20,3584]{3,2,1,0:T(8,128)(2,1)} %bitcast.166), calls=%async_computation.2 | async-start | bytes 5505024 | tf_op jit(solution)/shard_map/all_to_all | solution.py:110
  512.4 3.3 copy-start.2
Sparse Core Ops, SparseCore 0:
  91.4 80.6 all-gather.6
  174.9 70.2 all-gather.4
  302.9 68.6 reduce-scatter.4
  373.7 68.5 reduce-scatter.2
